TPU v7x, 32 devices: a whole 2x2x4 slice. The times are simulated.
32 devices in a mesh: gx: 4 (over z), gy: 2 (over x), gz: 4 (over y, core).
Axes of the slice: x: 2, y: 2, z: 4, core: 2. Of those that a mesh axis runs over, the one named last changes fastest.
Arguments:
- bases: float32 [4, 2, 4, 1024, 128], P('gx', 'gy', 'gz'), may hold values from -1 to 1, as said below
- ranks: int32 [4, 2, 4], P('gx', 'gy', 'gz'), may hold values from 64 to 128
- couplings: bfloat16 [4, 2, 4, 5, 1024, 1024], P('gx', 'gy', 'gz'), may hold values from -6 to 6
- vectors: float32 [4, 2, 4, 1024, 256], P('gx', 'gy', 'gz'), may hold values from -0.1875 to 0.1875
Outputs:
- projected: float32 [4, 2, 4, 5, 128, 128], P('gx', 'gy', 'gz')
- applied: float32 [4, 2, 4, 1024, 256], P('gx', 'gy', 'gz')
Inputs may be any that keep to these rules, and one draw needn't show every extreme that they name: `bases`: for each subdomain the 1024 x 128 matrix has orthonormal columns.
All inputs are finite; a program needn't handle non-finite values.
Results may differ from a plain program's by a relative error of at most 0.0003.
Values sent between devices are 32-bit elements; how exact they have to be, the bound alone decides.
A program may use at most 64 MiB of HBM per device.

v0:
```python
import jax
import jax.numpy as jnp
from jax import lax
from jax.sharding import PartitionSpec as P

OFFSET_LIST = ((1, 0, 0), (0, 1, 0), (0, 0, 1), (1, 1, 0), (1, 0, 1), (0, 1, 1), (1, 1, 1))


def passed_along(value, axis, by):
    length = lax.axis_size(axis)
    pairs = [(i, i + by) for i in range(length) if 0 <= i + by < length]
    return lax.ppermute(value, axis, pairs)


def move_x(value):
    return passed_along(value, "gx", -1)


def move_y(value):
    return passed_along(value, "gy", -1)


def move_z(value):
    return passed_along(value, "gz", -1)


def local(bases, ranks, couplings, vectors):
    width = bases.shape[-1]
    blocks = couplings.shape[3]
    columns = jnp.arange(width, dtype=jnp.int32)
    keep = (columns < ranks[..., None]).astype(jnp.float32)
    own_basis = bases[0, 0, 0] * keep[0, 0, 0][None, :]
    own_joined = jnp.concatenate([own_basis, vectors[0, 0, 0]], axis=-1)
    used = OFFSET_LIST[:blocks]
    left_parts = [
        jnp.dot(
            own_basis.T,
            couplings[0, 0, 0, slot].astype(jnp.float32),
            precision=lax.Precision.HIGHEST,
        )
        for slot in range(blocks)
    ]
    received = {}
    for offset in used:
        value = own_joined
        if offset[0] == 1:
            value = move_x(value)
        if offset[1] == 1:
            value = move_y(value)
        if offset[2] == 1:
            value = move_z(value)
        received[offset] = value
    results = []
    applied = jnp.zeros((own_basis.shape[0], vectors.shape[-1]), jnp.float32)
    for slot in range(blocks):
        neighbour = received[used[slot]]
        coupling = couplings[0, 0, 0, slot].astype(jnp.float32)
        applied = applied + jnp.dot(coupling, neighbour[:, width:], precision=lax.Precision.HIGHEST)
        block = jnp.dot(left_parts[slot], neighbour[:, :width], precision=lax.Precision.HIGHEST)
        results.append(block)
    stacked = jnp.stack(results, axis=0)
    return (
        stacked.reshape(1, 1, 1, blocks, width, width),
        applied.reshape(1, 1, 1, applied.shape[0], applied.shape[1]),
    )


def solution(mesh):
    return jax.shard_map(
        local,
        mesh=mesh,
        in_specs=(
            P("gx", "gy", "gz", None, None),
            P("gx", "gy", "gz"),
            P("gx", "gy", "gz", None, None, None),
            P("gx", "gy", "gz", None, None),
        ),
        out_specs=(P("gx", "gy", "gz", None, None, None), P("gx", "gy", "gz", None, None)),
        check_vma=False,
    )
```

profile of v0, /device:TPU:0, one launch (start us, length us, event | category | flops | bytes accessed | tf_op | source)
XLA Modules:
  0.0 91.3 jit_solution(15470665659506494645)
XLA Ops:
  1.3 0.0 copy-start
  1.3 1.2 %bitcast_multiply_fusion = f32[1024,128]{1,0:T(8,128)S(1)} fusion(f32[1,1,1,1024,128]{4,3,2,1,0:T(8,128)} %param.4, f32[128]{0:T(128)S(1)} %compare_convert_fusion), kind=kLoop, calls=%fused_computation.56 | loop fusion | flops 131072 | bytes 1049088 | tf_op jit(solution)/shard_map/mul | solution.py:32
  2.5 1.6 %pad_maximum_fusion = f32[1024,384]{1,0:T(8,128)S(1)} fusion(f32[1024,256]{1,0:T(8,128)} %bitcast.81, f32[1024,128]{1,0:T(8,128)S(1)} %bitcast_multiply_fusion), kind=kLoop, calls=%fused_computation.30 | loop fusion | flops 393216 | bytes 3145728 | tf_op jit(solution)/shard_map/concatenate | solution.py:33
  4.1 1.4 %collective-permute-start = (f32[1024,384]{1,0:T(8,128)S(1)}, f32[1024,384]{1,0:T(8,128)S(1)}, u32[]{:S(2)}, u32[]{:S(2)}) collective-permute-start(f32[1024,384]{1,0:T(8,128)S(1)} %pad_maximum_fusion), channel_id=1, source_target_pairs={{8,0},{16,8},{24,16},{9,1},{17,9},{25,17},{10,2},{18,10},{26,18},{... | collective-permute-start | bytes 4718600 | tf_op jit(solution)/shard_map/ppermute | solution.py:12
  5.5 1.3 %collective-permute-start.1 = (f32[1024,384]{1,0:T(8,128)S(1)}, f32[1024,384]{1,0:T(8,128)S(1)}, u32[]{:S(2)}, u32[]{:S(2)}) collective-permute-start(f32[1024,384]{1,0:T(8,128)S(1)} %pad_maximum_fusion), channel_id=1, source_target_pairs={{4,0},{5,1},{6,2},{7,3},{12,8},{13,9},{14,10},{15,11},{20,16},{21,... | collective-permute-start | bytes 4718600 | tf_op jit(solution)/shard_map/ppermute | solution.py:12
  6.8 1.3 %collective-permute-start.2 = (f32[1024,384]{1,0:T(8,128)S(1)}, f32[1024,384]{1,0:T(8,128)S(1)}, u32[]{:S(2)}, u32[]{:S(2)}) collective-permute-start(f32[1024,384]{1,0:T(8,128)S(1)} %pad_maximum_fusion), channel_id=1, source_target_pairs={{1,0},{2,1},{3,2},{5,4},{6,5},{7,6},{9,8},{10,9},{11,10},{13,12},{... | collective-permute-start | bytes 4718600 | tf_op jit(solution)/shard_map/ppermute | solution.py:12
  8.1 2.9 %fusion.18 = f32[128,1024]{1,0:T(8,128)S(1)} fusion(bf16[1,1,1,5,1024,1024]{5,4,3,2,1,0:T(8,128)(2,1)} %param.6, f32[1,1,1,1024,128]{4,3,2,1,0:T(8,128)} %param.4, f32[128]{0:T(128)S(1)} %compare_convert_fusion), kind=kOutput, calls=%fused_computation.18 | convolution fusion | flops 1610743808 | bytes 3146240 | tf_op jit(solution)/shard_map/dot_general | solution.py:36
  11.0 2.9 %fusion.14 = f32[128,1024]{1,0:T(8,128)S(1)} fusion(bf16[1,1,1,5,1024,1024]{5,4,3,2,1,0:T(8,128)(2,1)} %param.6, f32[1,1,1,1024,128]{4,3,2,1,0:T(8,128)} %param.4, f32[128]{0:T(128)S(1)} %compare_convert_fusion), kind=kOutput, calls=%fused_computation.14 | convolution fusion | flops 1610743808 | bytes 3146240 | tf_op jit(solution)/shard_map/dot_general | solution.py:36
  13.9 0.0 copy-start.1
  13.9 2.2 %fusion.10 = f32[128,1024]{1,0:T(8,128)S(1)} fusion(bf16[1,1,1,5,1024,1024]{5,4,3,2,1,0:T(8,128)(2,1)S(1)} %copy-done, f32[1,1,1,1024,128]{4,3,2,1,0:T(8,128)} %param.4, f32[128]{0:T(128)S(1)} %compare_convert_fusion), kind=kOutput, calls=%fused_computation.10 | convolution fusion | flops 1610743808 | bytes 3146240 | tf_op jit(solution)/shard_map/dot_general | solution.py:36
  16.2 1.1 %fusion.6 = f32[128,1024]{1,0:T(8,128)S(1)} fusion(bf16[1,1,1,5,1024,1024]{5,4,3,2,1,0:T(8,128)(2,1)S(1)} %copy-done, f32[1,1,1,1024,128]{4,3,2,1,0:T(8,128)S(1)} %copy-done.1, f32[128]{0:T(128)S(1)} %compare_convert_fusion), kind=kOutput, calls=%fused_computation.6 | convolution fusion | flops 1610743808 | bytes 3146240 | tf_op jit(solution)/shard_map/dot_general | solution.py:36
  17.3 1.1 %fusion.2 = f32[128,1024]{1,0:T(8,128)S(1)} fusion(bf16[1,1,1,5,1024,1024]{5,4,3,2,1,0:T(8,128)(2,1)S(1)} %copy-done, f32[1,1,1,1024,128]{4,3,2,1,0:T(8,128)S(1)} %copy-done.1, f32[128]{0:T(128)S(1)} %compare_convert_fusion), kind=kOutput, calls=%fused_computation.2 | convolution fusion | flops 1610743808 | bytes 3146240 | tf_op jit(solution)/shard_map/dot_general | solution.py:36
  18.4 25.1 %collective-permute-done = f32[1024,384]{1,0:T(8,128)S(1)} collective-permute-done((f32[1024,384]{1,0:T(8,128)S(1)}, f32[1024,384]{1,0:T(8,128)S(1)}, u32[]{:S(2)}, u32[]{:S(2)}) %collective-permute-start) | collective-permute-done | bytes 1572896 | tf_op jit(solution)/shard_map/ppermute | solution.py:12
  43.6 1.3 %collective-permute-start.3 = (f32[1024,384]{1,0:T(8,128)S(1)}, f32[1024,384]{1,0:T(8,128)}, u32[]{:S(2)}, u32[]{:S(2)}) collective-permute-start(f32[1024,384]{1,0:T(8,128)S(1)} %collective-permute-done), channel_id=1, source_target_pairs={{4,0},{5,1},{6,2},{7,3},{12,8},{13,9},{14,10},{15,11},{20,16},{21,... | collective-permute-start | bytes 4718600 | tf_op jit(solution)/shard_map/ppermute | solution.py:12
  44.9 1.5 %collective-permute-start.4 = (f32[1024,384]{1,0:T(8,128)S(1)}, f32[1024,384]{1,0:T(8,128)S(1)}, u32[]{:S(2)}, u32[]{:S(2)}) collective-permute-start(f32[1024,384]{1,0:T(8,128)S(1)} %collective-permute-done), channel_id=1, source_target_pairs={{1,0},{2,1},{3,2},{5,4},{6,5},{7,6},{9,8},{10,9},{11,10},{13,12},{... | collective-permute-start | bytes 4718600 | tf_op jit(solution)/shard_map/ppermute | solution.py:12
  46.3 0.6 fusion.49
  47.0 0.0 collective-permute-done.1
  47.0 0.6 fusion.48
  47.6 0.0 collective-permute-done.2
  47.7 0.6 fusion.47
  48.3 3.5 %fusion.8 = f32[256,1024]{1,0:T(8,128)S(1)} fusion(bf16[1,1,1,5,1024,1024]{5,4,3,2,1,0:T(8,128)(2,1)S(1)} %copy-done, f32[1024,384]{1,0:T(8,128)S(1)} %collective-permute-done.2), kind=kOutput, calls=%fused_computation.8 | convolution fusion | flops 3221225472 | bytes 4194304 | tf_op jit(solution)/shard_map/dot_general | solution.py:58
  51.8 3.6 %fusion.12 = f32[256,1024]{1,0:T(8,128)S(1)} fusion(bf16[1,1,1,5,1024,1024]{5,4,3,2,1,0:T(8,128)(2,1)S(1)} %copy-done, f32[1024,384]{1,0:T(8,128)S(1)} %collective-permute-done.1), kind=kOutput, calls=%fused_computation.12 | convolution fusion | flops 3221225472 | bytes 4194304 | tf_op jit(solution)/shard_map/dot_general | solution.py:58
  55.4 3.5 %fusion.42 = f32[256,1024]{1,0:T(8,128)S(1)} fusion(f32[256,1024]{1,0:T(8,128)S(1)} %fusion.8, f32[256,1024]{1,0:T(8,128)S(1)} %fusion.12, bf16[1,1,1,5,1024,1024]{5,4,3,2,1,0:T(8,128)(2,1)S(1)} %copy-done, f32[1024,384]{1,0:T(8,128)S(1)} %collective-permute-done), kind=kOutput, calls=%fused_computation.35 | convolution fusion | flops 3221749760 | bytes 6291456 | tf_op jit(solution)/shard_map/dot_general | solution.py:58
  58.9 0.0 collective-permute-done.4
  58.9 3.7 %fusion = f32[256,1024]{1,0:T(8,128)S(1)} fusion(bf16[1,1,1,5,1024,1024]{5,4,3,2,1,0:T(8,128)(2,1)S(1)} %copy-done, f32[1024,384]{1,0:T(8,128)S(1)} %collective-permute-done.4), kind=kOutput, calls=%fused_computation | convolution fusion | flops 3221225472 | bytes 4194304 | tf_op jit(solution)/shard_map/dot_general | solution.py:58
  62.7 18.5 %collective-permute-done.3 = f32[1024,384]{1,0:T(8,128)} collective-permute-done((f32[1024,384]{1,0:T(8,128)S(1)}, f32[1024,384]{1,0:T(8,128)}, u32[]{:S(2)}, u32[]{:S(2)}) %collective-permute-start.3) | collective-permute-done | bytes 1572896 | tf_op jit(solution)/shard_map/ppermute | solution.py:12
  81.1 4.8 %fusion.39 = f32[1,1,1,1024,256]{3,4,2,1,0:T(8,128)S(1)} fusion(f32[256,1024]{1,0:T(8,128)S(1)} %fusion, f32[256,1024]{1,0:T(8,128)S(1)} %fusion.42, bf16[1,1,1,5,1024,1024]{5,4,3,2,1,0:T(8,128)(2,1)S(1)} %copy-done, f32[1024,384]{1,0:T(8,128)} %collective-permute-done.3), kind=kOutput, calls=%fused_computation.34 | convolution fusion | flops 3221749760 | bytes 6291456 | tf_op jit(solution)/shard_map/dot_general | solution.py:58
  85.9 1.3 %copy.6 = f32[1,1,1,1024,256]{4,3,2,1,0:T(8,128)} copy(f32[1,1,1,1024,256]{3,4,2,1,0:T(8,128)S(1)} %fusion.39) | data formatting | bytes 2097152
  87.2 1.7 %fusion.46 = f32[5,128,128]{2,1,0:T(8,128)S(1)} fusion(f32[5,128,128]{2,1,0:T(8,128)S(1)} %fusion.47, f32[128,1024]{1,0:T(8,128)S(1)} %fusion.6, f32[1024,384]{1,0:T(8,128)} %collective-permute-done.3), kind=kOutput, calls=%fused_computation.39 | convolution fusion | flops 201326592 | bytes 1114112 | tf_op jit(solution)/shard_map/dot_general | solution.py:59
  88.9 1.7 %fusion.45 = f32[5,128,128]{2,1,0:T(8,128)S(1)} fusion(f32[5,128,128]{2,1,0:T(8,128)S(1)} %fusion.46, f32[128,1024]{1,0:T(8,128)S(1)} %fusion.2, f32[1024,384]{1,0:T(8,128)} %copy-done.2), kind=kOutput, calls=%fused_computation.37 | convolution fusion | flops 201326592 | bytes 1114112 | tf_op jit(solution)/shard_map/dot_general | solution.py:59
  90.6 0.0 copy-start.3
  90.6 0.7 copy-done.3
  (5 shorter events, 0.0 us)
Async XLA Ops:
  1.3 12.6 %copy-start = (bf16[1,1,1,5,1024,1024]{5,4,3,2,1,0:T(8,128)(2,1)S(1)}, bf16[1,1,1,5,1024,1024]{5,4,3,2,1,0:T(8,128)(2,1)}, u32[]{:S(2)}) copy-start(bf16[1,1,1,5,1024,1024]{5,4,3,2,1,0:T(8,128)(2,1)} %param.6) | copy-start | bytes 31457284
  4.1 39.5 %collective-permute-start = (f32[1024,384]{1,0:T(8,128)S(1)}, f32[1024,384]{1,0:T(8,128)S(1)}, u32[]{:S(2)}, u32[]{:S(2)}) collective-permute-start(f32[1024,384]{1,0:T(8,128)S(1)} %pad_maximum_fusion), channel_id=1, source_target_pairs={{8,0},{16,8},{24,16},{9,1},{17,9},{25,17},{10,2},{18,10},{26,18},{... | collective-permute-start | bytes 4718600 | tf_op jit(solution)/shard_map/ppermute | solution.py:12
  5.5 41.5 %collective-permute-start.1 = (f32[1024,384]{1,0:T(8,128)S(1)}, f32[1024,384]{1,0:T(8,128)S(1)}, u32[]{:S(2)}, u32[]{:S(2)}) collective-permute-start(f32[1024,384]{1,0:T(8,128)S(1)} %pad_maximum_fusion), channel_id=1, source_target_pairs={{4,0},{5,1},{6,2},{7,3},{12,8},{13,9},{14,10},{15,11},{20,16},{21,... | collective-permute-start | bytes 4718600 | tf_op jit(solution)/shard_map/ppermute | solution.py:12
  6.8 40.8 %collective-permute-start.2 = (f32[1024,384]{1,0:T(8,128)S(1)}, f32[1024,384]{1,0:T(8,128)S(1)}, u32[]{:S(2)}, u32[]{:S(2)}) collective-permute-start(f32[1024,384]{1,0:T(8,128)S(1)} %pad_maximum_fusion), channel_id=1, source_target_pairs={{1,0},{2,1},{3,2},{5,4},{6,5},{7,6},{9,8},{10,9},{11,10},{13,12},{... | collective-permute-start | bytes 4718600 | tf_op jit(solution)/shard_map/ppermute | solution.py:12
  13.9 2.3 %copy-start.1 = (f32[1,1,1,1024,128]{4,3,2,1,0:T(8,128)S(1)}, f32[1,1,1,1024,128]{4,3,2,1,0:T(8,128)}, u32[]{:S(2)}) copy-start(f32[1,1,1,1024,128]{4,3,2,1,0:T(8,128)} %param.4) | copy-start | bytes 1572868
  43.6 37.5 %collective-permute-start.3 = (f32[1024,384]{1,0:T(8,128)S(1)}, f32[1024,384]{1,0:T(8,128)}, u32[]{:S(2)}, u32[]{:S(2)}) collective-permute-start(f32[1024,384]{1,0:T(8,128)S(1)} %collective-permute-done), channel_id=1, source_target_pairs={{4,0},{5,1},{6,2},{7,3},{12,8},{13,9},{14,10},{15,11},{20,16},{21,... | collective-permute-start | bytes 4718600 | tf_op jit(solution)/shard_map/ppermute | solution.py:12
  44.9 14.0 %collective-permute-start.4 = (f32[1024,384]{1,0:T(8,128)S(1)}, f32[1024,384]{1,0:T(8,128)S(1)}, u32[]{:S(2)}, u32[]{:S(2)}) collective-permute-start(f32[1024,384]{1,0:T(8,128)S(1)} %collective-permute-done), channel_id=1, source_target_pairs={{1,0},{2,1},{3,2},{5,4},{6,5},{7,6},{9,8},{10,9},{11,10},{13,12},{... | collective-permute-start | bytes 4718600 | tf_op jit(solution)/shard_map/ppermute | solution.py:12
  58.9 22.2 %copy-start.2 = (f32[1024,384]{1,0:T(8,128)}, f32[1024,384]{1,0:T(8,128)S(1)}, u32[]{:S(2)}) copy-start(f32[1024,384]{1,0:T(8,128)S(1)} %collective-permute-done.4) | copy-start | bytes 4718596
  90.6 0.7 copy-start.3
where the time goes:
time: 91.7 us; the launch traced here: 91.3 us
  waiting for transfers between devices  43.6 us (48%)
  matrix products  34.6 us (38%)
  starting transfers between devices  6.76 us (7%)
  other arithmetic  2.8 us (3%)
  local copies, waits for them, and re-layouts  2.04 us (2%)
  between operations  1.51 us (2%)
    ppermute x5, waiting for transfers between devices, passed_along(): return lax.ppermute(value, axis, pairs)  43.6 us
    dot_general x5, matrix products, local(): jnp.dot(coupling, neighbour[:, width:], precision=lax.Precision.HIGHEST)  19.1 us
    dot_general x5, matrix products, local(): jnp.dot(own_basis.T, couplings[0, 0, 0, slot].astype(jnp.float32), precis...  10.2 us
    ppermute x5, starting transfers between devices, passed_along(): return lax.ppermute(value, axis, pairs)  6.76 us
    dot_general x5, matrix products, local(): jnp.dot(left_parts[slot], neighbour[:, :width], precision=lax.Precision.H...  5.27 us
    unnamed x9, local copies, waits for them, and re-layouts  2.04 us
  transfers between devices with their start and end apart: 5, of which 2 were waited for; matrix products, arithmetic and copies ran while one was open for 29% of the time, Pallas kernels for 0%

commit v1 on v0

v1 whole, which is shorter than its diff:
```python
import functools

import jax
import jax.numpy as jnp
from jax import lax
from jax.experimental import pallas as pl
from jax.experimental.pallas import tpu as pltpu
from jax.sharding import PartitionSpec as P

OFFSET_LIST = ((1, 0, 0), (0, 1, 0), (0, 0, 1), (1, 1, 0), (1, 0, 1), (0, 1, 1), (1, 1, 1))
AXES = ("gx", "gy", "gz")
X, Y, Z, XY, XZ = range(5)
LEFT_ORDER = (XY, Y, X, XZ, Z)


def split2(value):
    high = value.astype(jnp.bfloat16)
    low = (value - high.astype(jnp.float32)).astype(jnp.bfloat16)
    return high, low


def dot32(left, right):
    return jnp.dot(left, right, preferred_element_type=jnp.float32)


def kernel(
    sizes, ranks_ref, bases_ref, couplings_ref, vectors_ref, projected_ref, applied_ref,
    basis, stacked, basis_parts, blocks, values, left_out, left_in, back_out, back_in, total,
    basis_sem, block_sem, value_send, value_recv, left_send, left_recv, back_send, back_recv,
):
    count, m, k = blocks.shape[0], basis.shape[0], basis.shape[1]
    r = total.shape[1]
    half = m // 2
    place = [lax.axis_index(name) for name in AXES]
    has_up = [p < n - 1 for p, n in zip(place, sizes)]
    has_down = [p > 0 for p in place]

    def every(flags, offset):
        out = None
        for flag, o in zip(flags, offset):
            if o:
                out = flag if out is None else jnp.logical_and(out, flag)
        return out

    up = [every(has_up, o) for o in OFFSET_LIST[:count]]
    down = [every(has_down, o) for o in OFFSET_LIST[:count]]

    def device(offset, sign):
        return {name: p + sign * o for name, p, o in zip(AXES, place, offset)}

    basis_copy = pltpu.make_async_copy(bases_ref, basis, basis_sem)
    basis_copy.start()
    block_copies = [
        pltpu.make_async_copy(couplings_ref.at[s], blocks.at[s], block_sem.at[s]) for s in range(count)
    ]
    for s in LEFT_ORDER:
        block_copies[s].start()

    barrier = pltpu.get_barrier_semaphore()
    partners = jnp.int32(0)
    for s in range(count):
        for flag, sign in ((up[s], 1), (down[s], -1)):
            partners = partners + flag.astype(jnp.int32)

            @pl.when(flag)
            def _():
                pl.semaphore_signal(
                    barrier, inc=1, device_id=device(OFFSET_LIST[s], sign), device_id_type=pl.DeviceIdType.MESH
                )

    pl.semaphore_wait(barrier, partners)

    def rows(part):
        return pl.ds(part * half, half)

    def remote(src, dst, send, recv, offset, sign):
        return pltpu.make_async_remote_copy(
            src_ref=src, dst_ref=dst, send_sem=send, recv_sem=recv,
            device_id=device(offset, sign), device_id_type=pl.DeviceIdType.MESH,
        )

    def value_copy(slot, part, source, offset):
        return remote(
            source.at[rows(part)], values.at[slot, rows(part)],
            value_send.at[slot, part], value_recv.at[slot, part], offset, -1,
        )

    sent = {}
    for s in (X, Y, Z):
        for part in (0, 1):
            sent[s, part] = (value_copy(s, part, vectors_ref, OFFSET_LIST[s]), down[s])
    sent[XY, 0] = (value_copy(XY, 0, values.at[X], OFFSET_LIST[Y]), jnp.logical_and(has_up[0], has_down[1]))
    sent[XY, 1] = (value_copy(XY, 1, values.at[Y], OFFSET_LIST[X]), jnp.logical_and(has_up[1], has_down[0]))
    for part in (0, 1):
        sent[XZ, part] = (
            value_copy(XZ, part, values.at[X], OFFSET_LIST[Z]), jnp.logical_and(has_up[0], has_down[2]),
        )

    def start(slot, part):
        copy, flag = sent[slot, part]
        pl.when(flag)(copy.start)

    def arrived(slot, part):
        pl.when(up[slot])(sent[slot, part][0].wait_recv)

    left_copies = [
        remote(left_out.at[s], left_in.at[s], left_send.at[s], left_recv.at[s], OFFSET_LIST[s], 1)
        for s in range(count)
    ]
    back_copies = [
        remote(back_out.at[s], back_in.at[s], back_send.at[s], back_recv.at[s], OFFSET_LIST[s], -1)
        for s in range(count)
    ]

    start(X, 0)
    start(Y, 1)
    start(Z, 0)
    start(X, 1)
    start(Y, 0)
    start(Z, 1)

    total[...] = jnp.zeros_like(total)
    back_in[...] = jnp.zeros_like(back_in)
    basis_copy.wait()
    columns = lax.broadcasted_iota(jnp.int32, (m, k), 1)
    masked = jnp.where(columns < ranks_ref[0], basis[...], 0.0)
    high, low = split2(masked)
    basis_parts[:, :k] = high
    basis_parts[:, k:] = low
    high, low = split2(masked.T)
    stacked[:k] = high
    stacked[k:] = low

    wide = min(512, m)
    for s in LEFT_ORDER:
        block_copies[s].wait()

        @pl.when(up[s])
        def _():
            @pl.loop(0, m // wide)
            def _(step):
                there = pl.ds(pl.multiple_of(step * wide, wide), wide)
                both = dot32(stacked[...], blocks[s, :, there])
                left_out[s, :, there] = both[:k] + both[k:]

            left_copies[s].start()

    tall = min(512, m)

    def apply(slot, part):
        @pl.when(up[slot])
        def _():
            high, low = split2(values[slot, rows(part)])
            pair = jnp.concatenate([high, low], axis=1)

            @pl.loop(0, m // tall)
            def _(step):
                there = pl.ds(pl.multiple_of(step * tall, tall), tall)
                both = dot32(blocks[slot, there, rows(part)], pair)
                total[there] += both[:, :r] + both[:, r:]

    def project(slot):
        @pl.when(down[slot])
        def _():
            left_copies[slot].wait_recv()
            high, low = split2(left_in[slot])
            first = dot32(high, basis_parts[...])
            second = dot32(low, basis_parts[:, :k])
            back_out[slot] = first[:, :k] + first[:, k:] + second
            back_copies[slot].start()

    arrived(X, 0)
    start(XY, 0)
    start(XZ, 0)
    arrived(Y, 1)
    start(XY, 1)
    arrived(Z, 0)
    arrived(Z, 1)
    apply(Z, 0)
    apply(Z, 1)
    apply(X, 0)
    apply(Y, 1)
    project(Z)
    project(Y)
    project(XY)
    arrived(X, 1)
    start(XZ, 1)
    arrived(Y, 0)
    apply(X, 1)
    apply(Y, 0)
    arrived(XZ, 0)
    apply(XZ, 0)
    project(X)
    arrived(XZ, 1)
    apply(XZ, 1)
    arrived(XY, 0)
    apply(XY, 0)
    arrived(XY, 1)
    apply(XY, 1)
    applied_ref[...] = total[...]
    project(XZ)
    for s in range(count):
        pl.when(up[s])(back_copies[s].wait_recv)
    projected_ref[...] = back_in[...]
    for s in range(count):
        for part in (0, 1):
            copy, flag = sent[s, part]
            pl.when(flag)(copy.wait_send)
        pl.when(up[s])(left_copies[s].wait_send)
        pl.when(down[s])(back_copies[s].wait_send)


def solution(mesh):
    sizes = tuple(mesh.shape[name] for name in AXES)

    def local(bases, ranks, couplings, vectors):
        m, k = bases.shape[-2:]
        count = couplings.shape[3]
        r = vectors.shape[-1]
        f32, bf16 = jnp.float32, jnp.bfloat16
        dma = pltpu.SemaphoreType.DMA
        projected, applied = pl.pallas_call(
            functools.partial(kernel, sizes),
            out_shape=(
                jax.ShapeDtypeStruct((count, k, k), f32),
                jax.ShapeDtypeStruct((m, r), f32),
            ),
            in_specs=[pl.BlockSpec(memory_space=pltpu.SMEM)] + [pl.BlockSpec(memory_space=pl.ANY)] * 3,
            out_specs=(pl.BlockSpec(memory_space=pltpu.VMEM),) * 2,
            scratch_shapes=[
                pltpu.VMEM((m, k), f32),
                pltpu.VMEM((2 * k, m), bf16),
                pltpu.VMEM((m, 2 * k), bf16),
                pltpu.VMEM((count, m, m), bf16),
                pltpu.VMEM((count, m, r), f32),
                pltpu.VMEM((count, k, m), f32),
                pltpu.VMEM((count, k, m), f32),
                pltpu.VMEM((count, k, k), f32),
                pltpu.VMEM((count, k, k), f32),
                pltpu.VMEM((m, r), f32),
                dma,
                dma((count,)),
                dma((count, 2)),
                dma((count, 2)),
                dma((count,)),
                dma((count,)),
                dma((count,)),
                dma((count,)),
            ],
            compiler_params=pltpu.CompilerParams(collective_id=0, has_side_effects=True),
        )(
            ranks.reshape(1),
            bases.reshape(m, k),
            couplings.reshape(count, m, m),
            vectors.reshape(m, r),
        )
        return (
            projected.reshape(1, 1, 1, count, k, k),
            applied.reshape(1, 1, 1, m, r),
        )

    return jax.shard_map(
        local,
        mesh=mesh,
        in_specs=(
            P("gx", "gy", "gz", None, None),
            P("gx", "gy", "gz"),
            P("gx", "gy", "gz", None, None, None),
            P("gx", "gy", "gz", None, None),
        ),
        out_specs=(P("gx", "gy", "gz", None, None, None), P("gx", "gy", "gz", None, None)),
        check_vma=False,
    )
```

time: 91.7 us -> 54.5 us (0.59)
  Pallas kernels: 0 us -> 49 us
  waiting for transfers between devices: 43.6 us -> 0 us
  matrix products: 34.6 us -> 0 us
  starting transfers between devices: 6.76 us -> 0 us
  other arithmetic: 2.8 us -> 0 us
  local copies, waits for them, and re-layouts: 2.04 us -> 3.98 us
    pallas_call x0 -> x1, Pallas kernels: none -> 49 us  [local(): pl.pallas_call(functools.partial(kernel, sizes), out_shape=(jax.ShapeDtyp...]
    ppermute x5 -> x0, waiting for transfers between devices: 43.6 us -> none  [passed_along(): return lax.ppermute(value, axis, pairs)]
    dot_general x15 -> x0, matrix products: 34.6 us -> none  [the longest x5 19.1 us: local(): jnp.dot(coupling, neighbour[:, width:], precision=lax.Precision.HIGHEST)]
    ppermute x5 -> x0, starting transfers between devices: 6.76 us -> none  [passed_along(): return lax.ppermute(value, axis, pairs)]
    unnamed x9 -> x2, local copies, waits for them, and re-layouts: 2.04 us -> 3.98 us
    concatenate x1 -> x0, other arithmetic: 1.56 us -> none  [local(): own_joined = jnp.concatenate([own_basis, vectors[0, 0, 0]], axis=-1)]
    mul x1 -> x0, other arithmetic: 1.23 us -> none  [local(): own_basis = bases[0, 0, 0] * keep[0, 0, 0][None, :]]
  transfers between devices with their start and end apart: 5 -> 0, of which waited for: 2 -> 0; matrix products, arithmetic and copies ran while one was open for 29% -> 0% of each run, Pallas kernels for 0% -> 0%
where the time goes in v1:
time: 54.5 us; the launch traced here: 54.3 us
  Pallas kernels  49 us (90%)
  local copies, waits for them, and re-layouts  3.98 us (7%)
  between operations  1.28 us (2%)
    pallas_call x1, Pallas kernels, local(): pl.pallas_call(functools.partial(kernel, sizes), out_shape=(jax.ShapeDtyp...  49 us
    unnamed x2, local copies, waits for them, and re-layouts  3.98 us

profile of v1, /device:TPU:0, one launch (start us, length us, event | category | flops | bytes accessed | tf_op | source)
XLA Modules:
  0.0 54.3 jit_solution(5554173469353176351)
XLA Ops:
  1.3 49.0 %shard_map.59 = (f32[5,128,128]{2,1,0:T(8,128)}, f32[1024,256]{1,0:T(8,128)}) custom-call(s32[1]{0:T(128)} %bitcast.6.ranks_ref, f32[1024,128]{1,0:T(8,128)} %bitcast.10, bf16[5,1024,1024]{2,1,0:T(8,128)(2,1)} %bitcast.7, f32[1024,256]{1,0:T(8,128)} %bitcast.8), custom_call_target="tpu_custom_call" | custom-call | tf_op jit(solution)/shard_map/pallas_call | solution.py:222
  50.3 1.7 %copy.9 = f32[1,1,1,5,128,128]{5,4,3,2,1,0:T(8,128)} copy(f32[1,1,1,5,128,128]{5,4,3,2,1,0:T(8,128)} %bitcast.11) | data formatting | bytes 655360
  52.0 2.3 %copy.10 = f32[1,1,1,1024,256]{4,3,2,1,0:T(8,128)} copy(f32[1,1,1,1024,256]{4,3,2,1,0:T(8,128)} %bitcast.9) | data formatting | bytes 2097152

commit v2 on v1

--- a/solution.py
+++ b/solution.py
@@ -25,11 +25,11 @@
 
 def kernel(
     sizes, ranks_ref, bases_ref, couplings_ref, vectors_ref, projected_ref, applied_ref,
-    basis, stacked, basis_parts, blocks, values, left_out, left_in, back_out, back_in, total,
-    basis_sem, block_sem, value_send, value_recv, left_send, left_recv, back_send, back_recv,
+    basis, stacked, basis_parts, blocks, values, left_out, left_in, relay, back_out, back_in,
+    basis_sem, block_sem, value_send, value_recv, left_send, left_recv, relay_send, relay_recv, back_send, back_recv,
 ):
     count, m, k = blocks.shape[0], basis.shape[0], basis.shape[1]
-    r = total.shape[1]
+    r = applied_ref.shape[1]
     half = m // 2
     place = [lax.axis_index(name) for name in AXES]
     has_up = [p < n - 1 for p, n in zip(place, sizes)]
@@ -103,8 +103,22 @@
     def arrived(slot, part):
         pl.when(up[slot])(sent[slot, part][0].wait_recv)
 
+    relays = [
+        remote(left_out.at[XY, part], relay.at[part], relay_send.at[part], relay_recv.at[part], OFFSET_LIST[s], 1)
+        for part, s in ((0, X), (1, Y))
+    ]
+    onward = [
+        remote(relay.at[part], left_in.at[XY, part], left_send.at[XY, part], left_recv.at[XY, part], OFFSET_LIST[s], 1)
+        for part, s in ((0, Y), (1, X))
+    ]
+    passed = (
+        ((relays[0], onward[0]), jnp.logical_and(has_down[0], has_up[1])),
+        ((relays[1], onward[1]), jnp.logical_and(has_down[1], has_up[0])),
+    )
     left_copies = [
-        remote(left_out.at[s], left_in.at[s], left_send.at[s], left_recv.at[s], OFFSET_LIST[s], 1)
+        relays if s == XY else [
+            remote(left_out.at[s], left_in.at[s], left_send.at[s, 0], left_recv.at[s, 0], OFFSET_LIST[s], 1)
+        ]
         for s in range(count)
     ]
     back_copies = [
@@ -119,11 +133,9 @@
     start(Y, 0)
     start(Z, 1)
 
-    total[...] = jnp.zeros_like(total)
-    back_in[...] = jnp.zeros_like(back_in)
     basis_copy.wait()
     columns = lax.broadcasted_iota(jnp.int32, (m, k), 1)
-    masked = jnp.where(columns < ranks_ref[0], basis[...], 0.0)
+    masked = jnp.where(columns < ranks_ref[0, 0, 0], basis[...], 0.0)
     high, low = split2(masked)
     basis_parts[:, :k] = high
     basis_parts[:, k:] = low
@@ -131,19 +143,32 @@
     stacked[:k] = high
     stacked[k:] = low
 
-    wide = min(512, m)
     for s in LEFT_ORDER:
         block_copies[s].wait()
 
         @pl.when(up[s])
         def _():
-            @pl.loop(0, m // wide)
-            def _(step):
-                there = pl.ds(pl.multiple_of(step * wide, wide), wide)
+            @pl.loop(0, 2)
+            def _(part):
+                there = pl.ds(pl.multiple_of(part * half, half), half)
                 both = dot32(stacked[...], blocks[s, :, there])
-                left_out[s, :, there] = both[:k] + both[k:]
-
-            left_copies[s].start()
+                left_out[s, part] = both[:k] + both[k:]
+
+            for copy in left_copies[s]:
+                copy.start()
+
+    applied_ref[...] = jnp.zeros_like(applied_ref)
+    for s in range(count):
+
+        @pl.when(jnp.logical_not(up[s]))
+        def _():
+            back_in[s] = jnp.zeros((k, k), jnp.float32)
+
+    for copy, flag in passed:
+        @pl.when(flag)
+        def _():
+            copy[0].wait_recv()
+            copy[1].start()
 
     tall = min(512, m)
 
@@ -157,16 +182,20 @@
             def _(step):
                 there = pl.ds(pl.multiple_of(step * tall, tall), tall)
                 both = dot32(blocks[slot, there, rows(part)], pair)
-                total[there] += both[:, :r] + both[:, r:]
+                applied_ref[there] += both[:, :r] + both[:, r:]
 
     def project(slot):
         @pl.when(down[slot])
         def _():
-            left_copies[slot].wait_recv()
-            high, low = split2(left_in[slot])
-            first = dot32(high, basis_parts[...])
-            second = dot32(low, basis_parts[:, :k])
-            back_out[slot] = first[:, :k] + first[:, k:] + second
+            for copy in onward if slot == XY else left_copies[slot]:
+                copy.wait_recv()
+            out = None
+            for part in (0, 1):
+                high, low = split2(left_in[slot, part])
+                first = dot32(high, basis_parts[rows(part)])
+                term = first[:, :k] + first[:, k:] + dot32(low, basis_parts[rows(part), :k])
+                out = term if out is None else out + term
+            back_out[slot] = out
             back_copies[slot].start()
 
     arrived(X, 0)
@@ -193,12 +222,11 @@
     project(X)
     arrived(XZ, 1)
     apply(XZ, 1)
+    project(XZ)
     arrived(XY, 0)
     apply(XY, 0)
     arrived(XY, 1)
     apply(XY, 1)
-    applied_ref[...] = total[...]
-    project(XZ)
     for s in range(count):
         pl.when(up[s])(back_copies[s].wait_recv)
     projected_ref[...] = back_in[...]
@@ -206,8 +234,11 @@
         for part in (0, 1):
             copy, flag = sent[s, part]
             pl.when(flag)(copy.wait_send)
-        pl.when(up[s])(left_copies[s].wait_send)
+        for copy in left_copies[s]:
+            pl.when(up[s])(copy.wait_send)
         pl.when(down[s])(back_copies[s].wait_send)
+    for copy, flag in passed:
+        pl.when(flag)(copy[1].wait_send)
 
 
 def solution(mesh):
@@ -222,10 +253,10 @@
         projected, applied = pl.pallas_call(
             functools.partial(kernel, sizes),
             out_shape=(
-                jax.ShapeDtypeStruct((count, k, k), f32),
-                jax.ShapeDtypeStruct((m, r), f32),
+                pltpu.VMEM((count, k, k), f32),
+                pltpu.VMEM((m, r), f32),
             ),
-            in_specs=[pl.BlockSpec(memory_space=pltpu.SMEM)] + [pl.BlockSpec(memory_space=pl.ANY)] * 3,
+            in_specs=[pl.BlockSpec(memory_space=pltpu.SMEM)] + [pl.BlockSpec(memory_space=pltpu.HBM)] * 3,
             out_specs=(pl.BlockSpec(memory_space=pltpu.VMEM),) * 2,
             scratch_shapes=[
                 pltpu.VMEM((m, k), f32),
@@ -233,23 +264,25 @@
                 pltpu.VMEM((m, 2 * k), bf16),
                 pltpu.VMEM((count, m, m), bf16),
                 pltpu.VMEM((count, m, r), f32),
-                pltpu.VMEM((count, k, m), f32),
-                pltpu.VMEM((count, k, m), f32),
+                pltpu.VMEM((count, 2, k, m // 2), f32),
+                pltpu.VMEM((count, 2, k, m // 2), f32),
+                pltpu.VMEM((2, k, m // 2), f32),
                 pltpu.VMEM((count, k, k), f32),
                 pltpu.VMEM((count, k, k), f32),
-                pltpu.VMEM((m, r), f32),
                 dma,
                 dma((count,)),
                 dma((count, 2)),
                 dma((count, 2)),
-                dma((count,)),
-                dma((count,)),
+                dma((count, 2)),
+                dma((count, 2)),
+                dma((2,)),
+                dma((2,)),
                 dma((count,)),
                 dma((count,)),
             ],
-            compiler_params=pltpu.CompilerParams(collective_id=0, has_side_effects=True),
+            compiler_params=pltpu.CompilerParams(collective_id=0, has_side_effects=True, vmem_limit_bytes=64000 << 10),
         )(
-            ranks.reshape(1),
+            ranks,
             bases.reshape(m, k),
             couplings.reshape(count, m, m),
             vectors.reshape(m, r),

time: 54.5 us -> 47.2 us (0.87)
  Pallas kernels: 49 us -> 43.6 us
  local copies, waits for them, and re-layouts: 3.98 us -> 1.7 us
    pallas_call x1, Pallas kernels: 49 us -> 43.6 us  [local(): pl.pallas_call(functools.partial(kernel, sizes), out_shape=(pltpu.VMEM((c...]
    unnamed x2, local copies, waits for them, and re-layouts: 3.98 us -> 1.7 us
where the time goes in v2:
time: 47.2 us; the launch traced here: 46.6 us
  Pallas kernels  43.6 us (92%)
  local copies, waits for them, and re-layouts  1.7 us (4%)
  between operations  1.28 us (3%)
    pallas_call x1, Pallas kernels, local(): pl.pallas_call(functools.partial(kernel, sizes), out_shape=(pltpu.VMEM((c...  43.6 us
    unnamed x2, local copies, waits for them, and re-layouts  1.7 us

profile of v2, /device:TPU:0, one launch (start us, length us, event | category | flops | bytes accessed | tf_op | source)
XLA Modules:
  0.0 46.6 jit_solution(819324025144111263)
XLA Ops:
  1.3 43.6 %shard_map.59 = (f32[5,128,128]{2,1,0:T(8,128)S(1)}, f32[1024,256]{1,0:T(8,128)S(1)}) custom-call(s32[1,1,1]{2,1,0:T(1,128)S(6)} %copy.10.ranks_ref, f32[1024,128]{1,0:T(8,128)} %bitcast.9, bf16[5,1024,1024]{2,1,0:T(8,128)(2,1)} %bitcast.7, f32[1024,256]{1,0:T(8,128)} %bitcast.8), custom_call_target="tpu_custom_call" | custom-call | tf_op jit(solution)/shard_map/pallas_call | solution.py:253
  44.9 0.7 %copy.8 = f32[1,1,1,5,128,128]{5,4,3,2,1,0:T(8,128)} copy(f32[1,1,1,5,128,128]{5,4,3,2,1,0:T(8,128)S(1)} %bitcast.6) | data formatting | bytes 655360
  45.6 1.0 %copy.9 = f32[1,1,1,1024,256]{4,3,2,1,0:T(8,128)} copy(f32[1,1,1,1024,256]{4,3,2,1,0:T(8,128)S(1)} %bitcast.5) | data formatting | bytes 2097152
